TPU v7x, 1024 devices: a whole 8x8x8 slice. The times are simulated.
1024 devices in a mesh: segment: 16 (over z_hi, x), dp: 8 (over z_lo, core), tensor: 8 (over y).
Axes of the slice: x: 8, y: 8, z: 8 (z_hi: 2, z_lo: 4; z = z_hi * 4 + z_lo), core: 2. Of those that a mesh axis runs over, the one named last changes fastest.
Arguments:
- acts: bfloat16 [16, 2048, 1024], P('segment', ('dp', 'tensor')), may hold values from -6 to 6
- norm_gain: float32 [16, 1024], P('segment'), may hold values from 0.1 to 1.9
- final_gain: float32 [1024], replicated, may hold values from 0.1 to 1.9
- w_query: bfloat16 [16, 1024, 8192], P('segment', None, 'tensor'), may hold values from -0.015625 to 0.015625
- w_key: bfloat16 [16, 1024, 8192], P('segment', None, 'tensor'), may hold values from -0.1875 to 0.1875
- w_value: bfloat16 [16, 1024, 8192], P('segment', None, 'tensor'), may hold values from -0.1875 to 0.1875
- w_out: bfloat16 [16, 8192, 1024], P('segment', 'tensor'), may hold values from -0.0625 to 0.0625
- cache: bfloat16 [16, 2, 2048, 8192], P('segment', None, 'dp', 'tensor'), may hold values from -6 to 6
Outputs:
- updated: bfloat16 [16, 2048, 1024], P('segment', ('dp', 'tensor'))
- fresh: bfloat16 [16, 2, 2048, 8192], P('segment', None, 'dp', 'tensor')
All inputs are finite; a program needn't handle non-finite values.
Results may differ from a plain program's by a relative error of at most 0.01.
Values may be sent and summed in bfloat16 or wider, within the bound.
No kernel may reach another device: no remote copies, remote signals or barrier semaphores. Data moves between devices by JAX's collectives and lax.ppermute only.
A program may use at most 64 MiB of HBM per device.

v0:
```python
import jax
import jax.numpy as jnp
from jax import lax
from jax.experimental import pallas as pl
from jax.experimental.pallas import tpu as pltpu
from jax.sharding import PartitionSpec as P

HDIM = 128


EPSILON = 1e-06

SEND_ORDER = (3, 2, 4, 1, 5, 0, 6, 7)


def dot(a, b):
    return jnp.dot(a, b, preferred_element_type=jnp.float32)


def normalize(wide, gain):
    scale = lax.rsqrt(jnp.mean(wide * wide, axis=-1, keepdims=True) + EPSILON)
    return (wide * scale * gain).astype(jnp.bfloat16)


def is_decoder():
    return lax.axis_index("segment") >= lax.axis_size("segment") // 2


def attention_kernel(rows, gain, w_query, w_key, w_value, w_out, cache, partial, made, kv, wk, wv, wo, queries, context, sems):
    decoder = is_decoder()
    encoder = jnp.logical_not(decoder)
    weights = [pltpu.make_async_copy(w_key, wk, sems.at[0]), pltpu.make_async_copy(w_value, wv, sems.at[1])]
    out_copy = pltpu.make_async_copy(w_out, wo, sems.at[2])
    kept = [pltpu.make_async_copy(cache.at[which], kv.at[which], sems.at[3 + which]) for which in range(2)]
    made_copies = [pltpu.make_async_copy(kv.at[which], made.at[which], sems.at[5 + which]) for which in range(2)]

    @pl.when(decoder)
    def _():
        for copy in kept:
            copy.start()

    @pl.when(encoder)
    def _():
        for copy in weights:
            copy.start()

    out_copy.start()
    normed = normalize(rows[...].astype(jnp.float32), gain[...])
    queries[...] = dot(normed, w_query[...]).astype(jnp.bfloat16)

    @pl.when(decoder)
    def _():
        for copy in kept:
            copy.wait()

    @pl.when(encoder)
    def _():
        for which, weight in enumerate((wk, wv)):
            weights[which].wait()
            kv[which] = dot(normed, weight[...]).astype(jnp.bfloat16)
            made_copies[which].start()

    for head in range(queries.shape[1] // HDIM):
        cols = slice(head * HDIM, (head + 1) * HDIM)
        scores = lax.dot_general(queries[:, cols], kv[0, :, cols], (((1,), (1,)), ((), ())), preferred_element_type=jnp.float32)
        weight = jnp.exp(scores - jnp.max(scores, axis=-1, keepdims=True))
        inverse = 1.0 / jnp.sum(weight, axis=-1, keepdims=True)
        context[:, cols] = (dot(weight.astype(jnp.bfloat16), kv[1, :, cols]) * inverse).astype(jnp.bfloat16)
    out_copy.wait()
    partial[...] = dot(context[...], wo[...]).astype(jnp.bfloat16)

    @pl.when(encoder)
    def _():
        for copy in made_copies:
            copy.wait()


NEAR = pl.BlockSpec(memory_space=pltpu.VMEM)
FAR = pl.BlockSpec(memory_space=pltpu.HBM)
PARAMS = pltpu.CompilerParams(vmem_limit_bytes=24 << 20)
EXCHANGE = pl.CostEstimate(flops=20_000_000_000, bytes_accessed=1 << 20, transcendentals=0)


def far(*arrays):
    return [pltpu.with_memory_space_constraint(x, pltpu.HBM) for x in arrays]


def spread_kernel(x, copies, sem):
    copy = pltpu.make_async_copy(x, copies.at[0], sem)
    copy.start()
    copy.wait()
    value = copies[0]
    for to in range(1, copies.shape[0]):
        copies[to] = value


def near_spread_kernel(x, copies):
    for to in range(copies.shape[0]):
        copies[to] = x[...]


def gathered_copies(x, axis, near):
    devices = lax.axis_size(axis)
    copies = pl.pallas_call(
        near_spread_kernel if near else spread_kernel,
        out_shape=jax.ShapeDtypeStruct((devices, *x.shape), x.dtype),
        in_specs=[NEAR if near else FAR],
        out_specs=NEAR,
        scratch_shapes=[] if near else [pltpu.SemaphoreType.DMA],
        compiler_params=PARAMS,
        cost_estimate=EXCHANGE,
        name="spread",
    )(x if near else far(x)[0])
    return lax.all_to_all(copies, axis, 0, 0, tiled=True)


def attention(rows, gain, w_query, w_key, w_value, w_out, cache):
    length, width = rows.shape
    bf16 = jnp.bfloat16
    inner = w_query.shape[1]
    return pl.pallas_call(
        attention_kernel,
        out_shape=(jax.ShapeDtypeStruct((length, width), bf16), jax.ShapeDtypeStruct((2, length, inner), bf16)),
        in_specs=[NEAR] * 3 + [FAR] * 4,
        out_specs=(NEAR, FAR),
        scratch_shapes=[
            pltpu.VMEM((2, length, inner), bf16),
            pltpu.VMEM(w_key.shape, bf16),
            pltpu.VMEM(w_value.shape, bf16),
            pltpu.VMEM(w_out.shape, bf16),
            pltpu.VMEM((length, inner), bf16),
            pltpu.VMEM((length, inner), bf16),
            pltpu.SemaphoreType.DMA((7,)),
        ],
        compiler_params=PARAMS,
        name="section_attention",
    )(rows, gain, w_query, *far(w_key, w_value, w_out, cache))


def residual_kernel(arrived, tokens, gain, updated, memory):
    branch = jnp.sum(arrived[...].astype(jnp.float32), axis=0)
    new = (tokens[...].astype(jnp.float32) + branch).astype(jnp.bfloat16)
    updated[...] = new
    memory[...] = normalize(new.astype(jnp.float32), gain[...])


def residual(arrived, tokens, gain):
    shape = jax.ShapeDtypeStruct(tokens.shape, tokens.dtype)
    return pl.pallas_call(
        residual_kernel,
        out_shape=(shape, shape),
        in_specs=[NEAR, NEAR, NEAR],
        out_specs=(NEAR, NEAR),
        compiler_params=PARAMS,
        name="residual_norm",
    )(arrived, tokens, gain)


def sum_kernel(arrived, tokens, updated):
    branch = jnp.sum(arrived[...].astype(jnp.float32), axis=0)
    updated[...] = (tokens[...].astype(jnp.float32) + branch).astype(jnp.bfloat16)


def residual_only(arrived, tokens):
    return pl.pallas_call(
        sum_kernel,
        out_shape=jax.ShapeDtypeStruct(tokens.shape, tokens.dtype),
        in_specs=[NEAR, NEAR],
        out_specs=NEAR,
        compiler_params=PARAMS,
        name="residual_only",
    )(arrived, tokens)


def memory_kernel(memory, w_key, w_value, fresh, kv, sems):
    pieces = []
    for which, weight in enumerate((w_key, w_value)):
        for part in range(2):
            span = (which, pl.ds(part * (kv.shape[1] // 2), kv.shape[1] // 2))
            copy = pltpu.make_async_copy(kv.at[span], fresh.at[span], sems.at[len(pieces)])
            kv[span] = dot(memory[span[1], :], weight[...]).astype(jnp.bfloat16)
            copy.start()
            pieces.append(copy)
    for copy in pieces:
        copy.wait()


def memory_pair(memory, w_key, w_value):
    shape = (2, memory.shape[0], w_key.shape[1])
    return pl.pallas_call(
        memory_kernel,
        out_shape=jax.ShapeDtypeStruct(shape, memory.dtype),
        in_specs=[NEAR, NEAR, NEAR],
        out_specs=FAR,
        scratch_shapes=[pltpu.VMEM(shape, memory.dtype), pltpu.SemaphoreType.DMA((4,))],
        compiler_params=PARAMS,
        name="memory_pair",
    )(memory, w_key, w_value)


def on_device(acts, norm_gain, final_gain, w_query, w_key, w_value, w_out, cache):
    return whole_section(acts[0], norm_gain, final_gain[None], w_query[0], w_key[0], w_value[0], w_out[0], cache[0])


def whole_section(tokens, norm_gain, final_gain, w_query, w_key, w_value, w_out, cache):
    rows, width = tokens.shape
    tensor = lax.axis_size("tensor")
    half = lax.axis_size("segment") // 2
    all_rows = gathered_copies(tokens, "tensor", False).reshape(tensor * rows, width)
    partial, made = attention(all_rows, norm_gain, w_query, w_key, w_value, w_out, cache)
    segment = lax.axis_index("segment")
    pieces = partial.reshape(tensor, rows, width)
    decoder = segment >= half

    def arrive():
        return lax.all_to_all(pieces, "tensor", 0, 0, tiled=True)

    new, memory_part = lax.cond(decoder, lambda: (tokens, tokens), lambda: residual(arrive(), tokens, final_gain))
    sends = []
    for to in SEND_ORDER:
        sends.append(lax.ppermute(memory_part, "segment", [(half - 1, half + to)]))
    new = lax.cond(decoder, lambda: residual_only(arrive(), tokens), lambda: new)
    mine = sends[0]
    for to, sent in zip(SEND_ORDER[1:], sends[1:]):
        mine = jnp.where(segment == half + to, sent, mine)

    def received():
        memory = gathered_copies(mine, "tensor", True).reshape(tensor * rows, width)
        return memory_pair(memory, w_key, w_value)

    fresh = lax.cond(decoder, received, lambda: made)
    return (new[None], fresh[None])


def solution(mesh):
    placed = (
        P("segment", ("dp", "tensor"), None),
        P("segment", None),
        P(),
        P("segment", None, "tensor"),
        P("segment", None, "tensor"),
        P("segment", None, "tensor"),
        P("segment", "tensor", None),
        P("segment", None, "dp", "tensor"),
    )
    return jax.shard_map(
        on_device,
        mesh=mesh,
        in_specs=placed,
        out_specs=(P("segment", ("dp", "tensor"), None), P("segment", None, "dp", "tensor")),
        check_vma=False,
    )
```

profile of v0, /device:TPU:896, one launch (start us, length us, event | category | flops | bytes accessed | tf_op | source)
XLA Modules:
  0.0 99.6 jit_solution(11756821103434333592)
XLA Ops:
  0.6 1.8 %spread.3 = bf16[8,32,1024]{2,1,0:T(8,128)(2,1)} custom-call(bf16[32,1024]{1,0:T(8,128)(2,1)} %bitcast.23), custom_call_target="tpu_custom_call" | custom-call | flops 20000000000 | bytes 1048576 | tf_op jit(solution)/shard_map/spread/pallas_call | solution.py:104
  2.5 7.7 %all-to-all-start.3 = ((bf16[8,32,1024]{2,1,0:T(8,128)(2,1)}), bf16[8,32,1024]{2,1,0:T(8,128)(2,1)S(1)}, u32[]{:S(2)}, u32[]{:S(2)}) async-start(bf16[8,32,1024]{2,1,0:T(8,128)(2,1)} %spread.3), calls=%async_computation.3 | async-start | bytes 1048576 | tf_op jit(solution)/shard_map/all_to_all | solution.py:114
  10.1 17.5 %all-to-all-done.3 = bf16[8,32,1024]{2,1,0:T(8,128)(2,1)S(1)} async-done(((bf16[8,32,1024]{2,1,0:T(8,128)(2,1)}), bf16[8,32,1024]{2,1,0:T(8,128)(2,1)S(1)}, u32[]{:S(2)}, u32[]{:S(2)}) %all-to-all-start.3) | async-done | bytes 524320 | tf_op jit(solution)/shard_map/all_to_all | solution.py:114
  27.6 0.0 copy-done
  27.7 3.7 %section_attention.1 = (bf16[256,1024]{1,0:T(8,128)(2,1)S(1)}, bf16[2,256,1024]{2,1,0:T(8,128)(2,1)}) custom-call(bf16[256,1024]{1,0:T(8,128)(2,1)S(1)} %bitcast.12, f32[1,1024]{1,0:T(1,128)S(1)} %copy-done.1, bf16[1024,1024]{1,0:T(8,128)(2,1)S(1)} %bitcast.13, bf16[1024,1024]{1,0:T(8,128)(2,1)} %bitcast.15, bf16[1024,1024]{1,0:T(8,128)(2,1)} %bitcast.17, ...), custom_call_target="tpu_custom_call" | custom-call | tf_op jit(solution)/shard_map/section_attention/pallas_call | solution.py:121
  31.4 0.0 copy-start.2
  31.5 0.8 collective-permute-start.7
  32.3 0.7 collective-permute-start.6
  32.9 1.3 %collective-permute-start.5 = (bf16[32,1024]{1,0:T(8,128)(2,1)S(1)}, bf16[32,1024]{1,0:T(8,128)(2,1)S(1)}, u32[]{:S(2)}, u32[]{:S(2)}) collective-permute-start(bf16[32,1024]{1,0:T(8,128)(2,1)S(1)} %get-tuple-element.118), channel_id=1, source_target_pairs={{448,512},{449,513},{450,514},{451,515},{452,516},{453,517},{454,5... | collective-permute-start | bytes 196616 | tf_op jit(solution)/shard_map/ppermute | solution.py:221
  34.2 0.7 collective-permute-start.4
  34.9 0.7 collective-permute-start.3
  35.6 0.0 collective-permute-done.7
  35.6 0.7 collective-permute-start.2
  36.3 0.0 collective-permute-done.6
  36.3 0.7 collective-permute-start.1
  37.0 21.3 %collective-permute-done.5 = bf16[32,1024]{1,0:T(8,128)(2,1)S(1)} collective-permute-done((bf16[32,1024]{1,0:T(8,128)(2,1)S(1)}, bf16[32,1024]{1,0:T(8,128)(2,1)S(1)}, u32[]{:S(2)}, u32[]{:S(2)}) %collective-permute-start.5) | collective-permute-done | bytes 65568 | tf_op jit(solution)/shard_map/ppermute | solution.py:221
  58.3 0.7 collective-permute-start
  58.9 19.5 %conditional.4 = (bf16[32,1024]{1,0:T(8,128)(2,1)S(1)}) conditional(s32[]{:T(128)} %convert_element_type.2, bf16[32,1024]{1,0:T(8,128)(2,1)S(1)} %get-tuple-element.116, (bf16[8,32,1024]{2,1,0:T(8,128)(2,1)S(1)}, bf16[32,1024]{1,0:T(8,128)(2,1)S(1)}) %tuple.138), branch_computations={%region_2.0_spmd, %region_3.0_spmd} | conditional | bytes 1048584 | solution.py:222
  58.9 19.4 %all_to_all.18.arrived = bf16[8,32,1024]{2,1,0:T(8,128)(2,1)S(1)} all-to-all(bf16[8,32,1024]{2,1,0:T(8,128)(2,1)S(1)} %get-tuple-element.96), channel_id=1, replica_groups=mesh['segment'=16,'dp'=8,'tensor'=8] {'tensor'}, dimensions={0} | all-to-all | bytes 1048576 | tf_op jit(solution)/shard_map/cond/branch_1_fun/all_to_all | solution.py:216
  78.3 0.1 residual_only.1
  78.4 0.0 copy-start.6
  78.4 0.0 collective-permute-done.4
  78.4 0.0 collective-permute-done.3
  78.4 0.0 collective-permute-done.2
  78.4 0.0 collective-permute-done.1
  78.4 0.0 collective-permute-done
  78.5 0.0 copy-done.2
  78.5 0.6 copy-done.6
  79.0 20.6 %conditional.5 = (bf16[2,256,1024]{2,1,0:T(8,128)(2,1)}) conditional(s32[]{:T(128)} %convert_element_type.2, bf16[2,256,1024]{2,1,0:T(8,128)(2,1)} %get-tuple-element.117, (s32[]{:T(128)}, bf16[32,1024]{1,0:T(8,128)(2,1)S(1)}, bf16[32,1024]{1,0:T(8,128)(2,1)S(1)}, bf16[32,1024]{1,0:T(8,128)(2,1)S(1)}, bf16[32,1024]{1,0:T(8,128)(2,1)S(1)}, ...), branch_computations={%region_4.5_spmd, %region_5.6_spmd} | conditional | flops 20000229376 | bytes 11075690 | solution.py:231
  79.1 0.0 copy-start.3
  79.1 18.5 %all_to_all.19 = bf16[8,32,1024]{2,1,0:T(8,128)(2,1)S(1)} all-to-all(bf16[8,32,1024]{2,1,0:T(8,128)(2,1)S(1)} %spread.2), channel_id=1, replica_groups=mesh['segment'=16,'dp'=8,'tensor'=8] {'tensor'}, dimensions={0} | all-to-all | bytes 1048576 | tf_op jit(solution)/shard_map/cond/branch_1_fun/all_to_all | solution.py:114
  97.6 2.0 %memory_pair.1 = bf16[2,256,1024]{2,1,0:T(8,128)(2,1)} custom-call(bf16[256,1024]{1,0:T(8,128)(2,1)S(1)} %bitcast.14, bf16[1024,1024]{1,0:T(8,128)(2,1)S(1)} %get-tuple-element.107.w_key, bf16[1024,1024]{1,0:T(8,128)(2,1)S(1)} %copy-done.3), custom_call_target="tpu_custom_call" | custom-call | tf_op jit(solution)/shard_map/cond/branch_1_fun/memory_pair/pallas_call | solution.py:190
  (13 shorter events, 0.1 us)
Async XLA Ops:
  0.6 27.0 %copy-start = (bf16[1,1024,1024]{2,1,0:T(8,128)(2,1)S(1)}, bf16[1,1024,1024]{2,1,0:T(8,128)(2,1)}, u32[]{:S(2)}) copy-start(bf16[1,1024,1024]{2,1,0:T(8,128)(2,1)} %param.17) | copy-start | bytes 6291460
  0.6 27.0 %copy-start.1 = (f32[1,1024]{1,0:T(1,128)S(1)}, f32[1,1024]{1,0:T(1,128)}, u32[]{:S(2)}) copy-start(f32[1,1024]{1,0:T(1,128)} %gain.1) | copy-start | bytes 12292
  2.5 25.2 %all-to-all-start.3 = ((bf16[8,32,1024]{2,1,0:T(8,128)(2,1)}), bf16[8,32,1024]{2,1,0:T(8,128)(2,1)S(1)}, u32[]{:S(2)}, u32[]{:S(2)}) async-start(bf16[8,32,1024]{2,1,0:T(8,128)(2,1)} %spread.3), calls=%async_computation.3 | async-start | bytes 1048576 | tf_op jit(solution)/shard_map/all_to_all | solution.py:114
  27.6 3.8 %copy-start.4 = (bf16[1,32,1024]{2,1,0:T(8,128)(2,1)S(1)}, bf16[1,32,1024]{2,1,0:T(8,128)(2,1)}, u32[]{:S(2)}) copy-start(bf16[1,32,1024]{2,1,0:T(8,128)(2,1)} %param.14) | copy-start | bytes 196612
  27.6 3.8 %copy-start.5 = (f32[1024]{0:T(1024)S(1)}, f32[1024]{0:T(1024)}, u32[]{:S(2)}) copy-start(f32[1024]{0:T(1024)} %param.16) | copy-start | bytes 12292
  31.4 47.1 %copy-start.2 = (bf16[1,1024,1024]{2,1,0:T(8,128)(2,1)S(1)}, bf16[1,1024,1024]{2,1,0:T(8,128)(2,1)}, u32[]{:S(2)}) copy-start(bf16[1,1024,1024]{2,1,0:T(8,128)(2,1)} %param.18) | copy-start | bytes 6291460
  31.5 4.1 %collective-permute-start.7 = (bf16[32,1024]{1,0:T(8,128)(2,1)S(1)}, bf16[32,1024]{1,0:T(8,128)(2,1)S(1)}, u32[]{:S(2)}, u32[]{:S(2)}) collective-permute-start(bf16[32,1024]{1,0:T(8,128)(2,1)S(1)} %get-tuple-element.118), channel_id=1, source_target_pairs={{448,960},{449,961},{450,962},{451,963},{452,964},{453,965},{454,9... | collective-permute-start | bytes 196616 | tf_op jit(solution)/shard_map/ppermute | solution.py:221
  32.3 4.0 %collective-permute-start.6 = (bf16[32,1024]{1,0:T(8,128)(2,1)S(1)}, bf16[32,1024]{1,0:T(8,128)(2,1)S(1)}, u32[]{:S(2)}, u32[]{:S(2)}) collective-permute-start(bf16[32,1024]{1,0:T(8,128)(2,1)S(1)} %get-tuple-element.118), channel_id=1, source_target_pairs={{448,896},{449,897},{450,898},{451,899},{452,900},{453,901},{454,9... | collective-permute-start | bytes 196616 | tf_op jit(solution)/shard_map/ppermute | solution.py:221
  32.9 25.3 %collective-permute-start.5 = (bf16[32,1024]{1,0:T(8,128)(2,1)S(1)}, bf16[32,1024]{1,0:T(8,128)(2,1)S(1)}, u32[]{:S(2)}, u32[]{:S(2)}) collective-permute-start(bf16[32,1024]{1,0:T(8,128)(2,1)S(1)} %get-tuple-element.118), channel_id=1, source_target_pairs={{448,512},{449,513},{450,514},{451,515},{452,516},{453,517},{454,5... | collective-permute-start | bytes 196616 | tf_op jit(solution)/shard_map/ppermute | solution.py:221
  34.2 44.2 %collective-permute-start.4 = (bf16[32,1024]{1,0:T(8,128)(2,1)S(1)}, bf16[32,1024]{1,0:T(8,128)(2,1)S(1)}, u32[]{:S(2)}, u32[]{:S(2)}) collective-permute-start(bf16[32,1024]{1,0:T(8,128)(2,1)S(1)} %get-tuple-element.118), channel_id=1, source_target_pairs={{448,832},{449,833},{450,834},{451,835},{452,836},{453,837},{454,8... | collective-permute-start | bytes 196616 | tf_op jit(solution)/shard_map/ppermute | solution.py:221
  34.9 43.5 %collective-permute-start.3 = (bf16[32,1024]{1,0:T(8,128)(2,1)S(1)}, bf16[32,1024]{1,0:T(8,128)(2,1)S(1)}, u32[]{:S(2)}, u32[]{:S(2)}) collective-permute-start(bf16[32,1024]{1,0:T(8,128)(2,1)S(1)} %get-tuple-element.118), channel_id=1, source_target_pairs={{448,576},{449,577},{450,578},{451,579},{452,580},{453,581},{454,5... | collective-permute-start | bytes 196616 | tf_op jit(solution)/shard_map/ppermute | solution.py:221
  35.6 42.8 %collective-permute-start.2 = (bf16[32,1024]{1,0:T(8,128)(2,1)S(1)}, bf16[32,1024]{1,0:T(8,128)(2,1)S(1)}, u32[]{:S(2)}, u32[]{:S(2)}) collective-permute-start(bf16[32,1024]{1,0:T(8,128)(2,1)S(1)} %get-tuple-element.118), channel_id=1, source_target_pairs={{448,768},{449,769},{450,770},{451,771},{452,772},{453,773},{454,7... | collective-permute-start | bytes 196616 | tf_op jit(solution)/shard_map/ppermute | solution.py:221
  36.3 42.2 %collective-permute-start.1 = (bf16[32,1024]{1,0:T(8,128)(2,1)S(1)}, bf16[32,1024]{1,0:T(8,128)(2,1)S(1)}, u32[]{:S(2)}, u32[]{:S(2)}) collective-permute-start(bf16[32,1024]{1,0:T(8,128)(2,1)S(1)} %get-tuple-element.118), channel_id=1, source_target_pairs={{448,704},{449,705},{450,706},{451,707},{452,708},{453,709},{454,7... | collective-permute-start | bytes 196616 | tf_op jit(solution)/shard_map/ppermute | solution.py:221
  58.3 20.2 %collective-permute-start = (bf16[32,1024]{1,0:T(8,128)(2,1)S(1)}, bf16[32,1024]{1,0:T(8,128)(2,1)S(1)}, u32[]{:S(2)}, u32[]{:S(2)}) collective-permute-start(bf16[32,1024]{1,0:T(8,128)(2,1)S(1)} %get-tuple-element.118), channel_id=1, source_target_pairs={{448,640},{449,641},{450,642},{451,643},{452,644},{453,645},{454,6... | collective-permute-start | bytes 196616 | tf_op jit(solution)/shard_map/ppermute | solution.py:221
  78.4 0.6 copy-start.6
  79.1 18.5 %copy-start.3 = (bf16[1024,1024]{1,0:T(8,128)(2,1)S(1)}, bf16[1024,1024]{1,0:T(8,128)(2,1)}, u32[]{:S(2)}) copy-start(bf16[1024,1024]{1,0:T(8,128)(2,1)} %get-tuple-element.108.w_value) | copy-start | bytes 6291460 | tf_op jit(solution)/shard_map/cond
where the time goes:
time: 100 us; the launch traced here: 99.6 us
  waiting for transfers between devices  38.8 us (39%)
  blocking collectives  37.8 us (38%)
  starting transfers between devices  13.7 us (14%)
  Pallas kernels  7.67 us (8%)
    ppermute x8, waiting for transfers between devices, whole_section(): sends.append(lax.ppermute(memory_part, 'segment', [(half - 1, half + to)]))  21.3 us
    all_to_all x1, blocking collectives, arrive(): return lax.all_to_all(pieces, 'tensor', 0, 0, tiled=True)  19.4 us
    all_to_all x1, blocking collectives, gathered_copies(): return lax.all_to_all(copies, axis, 0, 0, tiled=True)  18.5 us
    all_to_all x1, waiting for transfers between devices, gathered_copies(): return lax.all_to_all(copies, axis, 0, 0, tiled=True)  17.5 us
    all_to_all x1, starting transfers between devices, gathered_copies(): return lax.all_to_all(copies, axis, 0, 0, tiled=True)  7.66 us
    ppermute x8, starting transfers between devices, whole_section(): sends.append(lax.ppermute(memory_part, 'segment', [(half - 1, half + to)]))  6.07 us
    pallas_call x1, Pallas kernels, attention(): pl.pallas_call(attention_kernel, out_shape=(jax.ShapeDtypeStruct((length,...  3.72 us
    pallas_call x1, Pallas kernels, memory_pair(): pl.pallas_call(memory_kernel, out_shape=jax.ShapeDtypeStruct(shape, memor...  2.01 us
  transfers between devices with their start and end apart: 9, of which 2 were waited for; matrix products, arithmetic and copies ran while one was open for 0% of the time, Pallas kernels for 0%

commit v1 on v0

--- a/solution.py
+++ b/solution.py
@@ -26,7 +26,7 @@
     return lax.axis_index("segment") >= lax.axis_size("segment") // 2
 
 
-def attention_kernel(rows, gain, w_query, w_key, w_value, w_out, cache, partial, made, kv, wk, wv, wo, queries, context, sems):
+def attention_kernel(rows, w_query, w_key, w_value, w_out, cache, partial, made, kv, wk, wv, wo, queries, context, sems):
     decoder = is_decoder()
     encoder = jnp.logical_not(decoder)
     weights = [pltpu.make_async_copy(w_key, wk, sems.at[0]), pltpu.make_async_copy(w_value, wv, sems.at[1])]
@@ -45,8 +45,7 @@
             copy.start()
 
     out_copy.start()
-    normed = normalize(rows[...].astype(jnp.float32), gain[...])
-    queries[...] = dot(normed, w_query[...]).astype(jnp.bfloat16)
+    queries[...] = dot(rows[...], w_query[...]).astype(jnp.bfloat16)
 
     @pl.when(decoder)
     def _():
@@ -57,8 +56,7 @@
     def _():
         for which, weight in enumerate((wk, wv)):
             weights[which].wait()
-            kv[which] = dot(normed, weight[...]).astype(jnp.bfloat16)
-            made_copies[which].start()
+            kv[which] = dot(rows[...], weight[...]).astype(jnp.bfloat16)
 
     for head in range(queries.shape[1] // HDIM):
         cols = slice(head * HDIM, (head + 1) * HDIM)
@@ -67,6 +65,12 @@
         inverse = 1.0 / jnp.sum(weight, axis=-1, keepdims=True)
         context[:, cols] = (dot(weight.astype(jnp.bfloat16), kv[1, :, cols]) * inverse).astype(jnp.bfloat16)
     out_copy.wait()
+
+    @pl.when(encoder)
+    def _():
+        for copy in made_copies:
+            copy.start()
+
     partial[...] = dot(context[...], wo[...]).astype(jnp.bfloat16)
 
     @pl.when(encoder)
@@ -85,43 +89,46 @@
     return [pltpu.with_memory_space_constraint(x, pltpu.HBM) for x in arrays]
 
 
-def spread_kernel(x, copies, sem):
-    copy = pltpu.make_async_copy(x, copies.at[0], sem)
-    copy.start()
-    copy.wait()
-    value = copies[0]
-    for to in range(1, copies.shape[0]):
-        copies[to] = value
-
-
-def near_spread_kernel(x, copies):
+def normed_spread_kernel(x, gain, copies, rows, gains, sems):
+    parts = [pltpu.make_async_copy(x, rows, sems.at[0]), pltpu.make_async_copy(gain, gains, sems.at[1])]
+    for copy in parts:
+        copy.start()
+    for copy in parts:
+        copy.wait()
+    normed = normalize(rows[...].astype(jnp.float32), gains[...])
+    for to in range(copies.shape[0]):
+        copies[to] = normed
+
+
+def spread_kernel(x, copies):
     for to in range(copies.shape[0]):
         copies[to] = x[...]
 
 
-def gathered_copies(x, axis, near):
+def gathered_copies(x, axis, gain=None):
     devices = lax.axis_size(axis)
+    rough = gain is not None
     copies = pl.pallas_call(
-        near_spread_kernel if near else spread_kernel,
+        normed_spread_kernel if rough else spread_kernel,
         out_shape=jax.ShapeDtypeStruct((devices, *x.shape), x.dtype),
-        in_specs=[NEAR if near else FAR],
+        in_specs=[FAR, FAR] if rough else [NEAR],
         out_specs=NEAR,
-        scratch_shapes=[] if near else [pltpu.SemaphoreType.DMA],
+        scratch_shapes=[pltpu.VMEM(x.shape, x.dtype), pltpu.VMEM(gain.shape, gain.dtype), pltpu.SemaphoreType.DMA((2,))] if rough else [],
         compiler_params=PARAMS,
         cost_estimate=EXCHANGE,
         name="spread",
-    )(x if near else far(x)[0])
+    )(*(far(x, gain) if rough else [x]))
     return lax.all_to_all(copies, axis, 0, 0, tiled=True)
 
 
-def attention(rows, gain, w_query, w_key, w_value, w_out, cache):
+def attention(rows, w_query, w_key, w_value, w_out, cache):
     length, width = rows.shape
     bf16 = jnp.bfloat16
     inner = w_query.shape[1]
     return pl.pallas_call(
         attention_kernel,
         out_shape=(jax.ShapeDtypeStruct((length, width), bf16), jax.ShapeDtypeStruct((2, length, inner), bf16)),
-        in_specs=[NEAR] * 3 + [FAR] * 4,
+        in_specs=[NEAR] * 2 + [FAR] * 4,
         out_specs=(NEAR, FAR),
         scratch_shapes=[
             pltpu.VMEM((2, length, inner), bf16),
@@ -134,7 +141,7 @@
         ],
         compiler_params=PARAMS,
         name="section_attention",
-    )(rows, gain, w_query, *far(w_key, w_value, w_out, cache))
+    )(rows, w_query, *far(w_key, w_value, w_out, cache))
 
 
 def residual_kernel(arrived, tokens, gain, updated, memory):
@@ -206,8 +213,8 @@
     rows, width = tokens.shape
     tensor = lax.axis_size("tensor")
     half = lax.axis_size("segment") // 2
-    all_rows = gathered_copies(tokens, "tensor", False).reshape(tensor * rows, width)
-    partial, made = attention(all_rows, norm_gain, w_query, w_key, w_value, w_out, cache)
+    all_rows = gathered_copies(tokens, "tensor", norm_gain).reshape(tensor * rows, width)
+    partial, made = attention(all_rows, w_query, w_key, w_value, w_out, cache)
     segment = lax.axis_index("segment")
     pieces = partial.reshape(tensor, rows, width)
     decoder = segment >= half
@@ -225,7 +232,7 @@
         mine = jnp.where(segment == half + to, sent, mine)
 
     def received():
-        memory = gathered_copies(mine, "tensor", True).reshape(tensor * rows, width)
+        memory = gathered_copies(mine, "tensor").reshape(tensor * rows, width)
         return memory_pair(memory, w_key, w_value)
 
     fresh = lax.cond(decoder, received, lambda: made)

time: 100 us -> 100 us (level)
  no operation moved by 1% of the time
where the time goes in v1:
time: 100 us; the launch traced here: 99.8 us
  waiting for transfers between devices  39.1 us (39%)
  blocking collectives  37.8 us (38%)
  starting transfers between devices  13.7 us (14%)
  Pallas kernels  7.67 us (8%)
    ppermute x8, waiting for transfers between devices, whole_section(): sends.append(lax.ppermute(memory_part, 'segment', [(half - 1, half + to)]))  21.6 us
    all_to_all x1, blocking collectives, arrive(): return lax.all_to_all(pieces, 'tensor', 0, 0, tiled=True)  19.4 us
    all_to_all x1, blocking collectives, gathered_copies(): return lax.all_to_all(copies, axis, 0, 0, tiled=True)  18.5 us
    all_to_all x1, waiting for transfers between devices, gathered_copies(): return lax.all_to_all(copies, axis, 0, 0, tiled=True)  17.5 us
    all_to_all x1, starting transfers between devices, gathered_copies(): return lax.all_to_all(copies, axis, 0, 0, tiled=True)  7.66 us
    ppermute x8, starting transfers between devices, whole_section(): sends.append(lax.ppermute(memory_part, 'segment', [(half - 1, half + to)]))  6.07 us
    pallas_call x1, Pallas kernels, attention(): pl.pallas_call(attention_kernel, out_shape=(jax.ShapeDtypeStruct((length,...  3.61 us
    pallas_call x1, Pallas kernels, memory_pair(): pl.pallas_call(memory_kernel, out_shape=jax.ShapeDtypeStruct(shape, memor...  2.01 us
  transfers between devices with their start and end apart: 9, of which 2 were waited for; matrix products, arithmetic and copies ran while one was open for 0% of the time, Pallas kernels for 0%

profile of v1, /device:TPU:896, one launch (start us, length us, event | category | flops | bytes accessed | tf_op | source)
XLA Modules:
  0.0 99.8 jit_solution(11498830794375554234)
XLA Ops:
  0.6 0.0 copy-start
  0.6 1.9 %spread.3 = bf16[8,32,1024]{2,1,0:T(8,128)(2,1)} custom-call(bf16[32,1024]{1,0:T(8,128)(2,1)} %bitcast.23, f32[1,1024]{1,0:T(1,128)} %gain.1), custom_call_target="tpu_custom_call" | custom-call | flops 20000000000 | bytes 1048576 | tf_op jit(solution)/shard_map/spread/pallas_call | solution.py:111
  2.6 7.7 %all-to-all-start.3 = ((bf16[8,32,1024]{2,1,0:T(8,128)(2,1)}), bf16[8,32,1024]{2,1,0:T(8,128)(2,1)S(1)}, u32[]{:S(2)}, u32[]{:S(2)}) async-start(bf16[8,32,1024]{2,1,0:T(8,128)(2,1)} %spread.3), calls=%async_computation.3 | async-start | bytes 1048576 | tf_op jit(solution)/shard_map/all_to_all | solution.py:121
  10.2 17.5 %all-to-all-done.3 = bf16[8,32,1024]{2,1,0:T(8,128)(2,1)S(1)} async-done(((bf16[8,32,1024]{2,1,0:T(8,128)(2,1)}), bf16[8,32,1024]{2,1,0:T(8,128)(2,1)S(1)}, u32[]{:S(2)}, u32[]{:S(2)}) %all-to-all-start.3) | async-done | bytes 524320 | tf_op jit(solution)/shard_map/all_to_all | solution.py:121
  27.7 3.6 %section_attention.1 = (bf16[256,1024]{1,0:T(8,128)(2,1)S(1)}, bf16[2,256,1024]{2,1,0:T(8,128)(2,1)}) custom-call(bf16[256,1024]{1,0:T(8,128)(2,1)S(1)} %bitcast.13, bf16[1024,1024]{1,0:T(8,128)(2,1)S(1)} %bitcast.12, bf16[1024,1024]{1,0:T(8,128)(2,1)} %bitcast.15, bf16[1024,1024]{1,0:T(8,128)(2,1)} %bitcast.17, bf16[1024,1024]{1,0:T(8,128)(2,1)} %bitcast.19, ...), custom_call_target="tpu_custom_call" | custom-call | tf_op jit(solution)/shard_map/section_attention/pallas_call | solution.py:128
  31.4 0.0 copy-start.1
  31.4 0.8 collective-permute-start.7
  32.2 0.7 collective-permute-start.6
  32.9 1.3 %collective-permute-start.5 = (bf16[32,1024]{1,0:T(8,128)(2,1)S(1)}, bf16[32,1024]{1,0:T(8,128)(2,1)S(1)}, u32[]{:S(2)}, u32[]{:S(2)}) collective-permute-start(bf16[32,1024]{1,0:T(8,128)(2,1)S(1)} %get-tuple-element.118), channel_id=1, source_target_pairs={{448,512},{449,513},{450,514},{451,515},{452,516},{453,517},{454,5... | collective-permute-start | bytes 196616 | tf_op jit(solution)/shard_map/ppermute | solution.py:228
  34.2 0.7 collective-permute-start.4
  34.9 0.7 collective-permute-start.3
  35.6 0.0 collective-permute-done.7
  35.6 0.7 collective-permute-start.2
  36.2 0.0 collective-permute-done.6
  36.3 0.7 collective-permute-start.1
  36.9 21.5 %collective-permute-done.5 = bf16[32,1024]{1,0:T(8,128)(2,1)S(1)} collective-permute-done((bf16[32,1024]{1,0:T(8,128)(2,1)S(1)}, bf16[32,1024]{1,0:T(8,128)(2,1)S(1)}, u32[]{:S(2)}, u32[]{:S(2)}) %collective-permute-start.5) | collective-permute-done | bytes 65568 | tf_op jit(solution)/shard_map/ppermute | solution.py:228
  58.5 0.7 collective-permute-start
  59.1 19.5 %conditional.4 = (bf16[32,1024]{1,0:T(8,128)(2,1)S(1)}) conditional(s32[]{:T(128)} %convert_element_type.2, bf16[32,1024]{1,0:T(8,128)(2,1)S(1)} %get-tuple-element.116, (bf16[8,32,1024]{2,1,0:T(8,128)(2,1)S(1)}, bf16[32,1024]{1,0:T(8,128)(2,1)S(1)}) %tuple.138), branch_computations={%region_2.0_spmd, %region_3.0_spmd} | conditional | bytes 1048584 | solution.py:229
  59.2 19.4 %all_to_all.18.arrived = bf16[8,32,1024]{2,1,0:T(8,128)(2,1)S(1)} all-to-all(bf16[8,32,1024]{2,1,0:T(8,128)(2,1)S(1)} %get-tuple-element.96), channel_id=1, replica_groups=mesh['segment'=16,'dp'=8,'tensor'=8] {'tensor'}, dimensions={0} | all-to-all | bytes 1048576 | tf_op jit(solution)/shard_map/cond/branch_1_fun/all_to_all | solution.py:223
  78.5 0.1 residual_only.1
  78.6 0.0 copy-start.5
  78.6 0.0 collective-permute-done.4
  78.6 0.0 collective-permute-done.3
  78.6 0.0 collective-permute-done.2
  78.6 0.0 collective-permute-done.1
  78.7 0.0 collective-permute-done
  78.7 0.6 copy-done.5
  79.2 20.6 %conditional.5 = (bf16[2,256,1024]{2,1,0:T(8,128)(2,1)}) conditional(s32[]{:T(128)} %convert_element_type.2, bf16[2,256,1024]{2,1,0:T(8,128)(2,1)} %get-tuple-element.117, (s32[]{:T(128)}, bf16[32,1024]{1,0:T(8,128)(2,1)S(1)}, bf16[32,1024]{1,0:T(8,128)(2,1)S(1)}, bf16[32,1024]{1,0:T(8,128)(2,1)S(1)}, bf16[32,1024]{1,0:T(8,128)(2,1)S(1)}, ...), branch_computations={%region_4.5_spmd, %region_5.6_spmd} | conditional | flops 20000229376 | bytes 11075690 | solution.py:238
  79.3 0.0 copy-start.2
  79.3 18.5 %all_to_all.19 = bf16[8,32,1024]{2,1,0:T(8,128)(2,1)S(1)} all-to-all(bf16[8,32,1024]{2,1,0:T(8,128)(2,1)S(1)} %spread.2), channel_id=1, replica_groups=mesh['segment'=16,'dp'=8,'tensor'=8] {'tensor'}, dimensions={0} | all-to-all | bytes 1048576 | tf_op jit(solution)/shard_map/cond/branch_1_fun/all_to_all | solution.py:121
  97.8 0.0 copy-done.2
  97.8 2.0 %memory_pair.1 = bf16[2,256,1024]{2,1,0:T(8,128)(2,1)} custom-call(bf16[256,1024]{1,0:T(8,128)(2,1)S(1)} %bitcast.14, bf16[1024,1024]{1,0:T(8,128)(2,1)S(1)} %get-tuple-element.107.w_key, bf16[1024,1024]{1,0:T(8,128)(2,1)S(1)} %copy-done.2), custom_call_target="tpu_custom_call" | custom-call | tf_op jit(solution)/shard_map/cond/branch_1_fun/memory_pair/pallas_call | solution.py:197
  (11 shorter events, 0.1 us)
Async XLA Ops:
  0.6 27.1 %copy-start = (bf16[1,1024,1024]{2,1,0:T(8,128)(2,1)S(1)}, bf16[1,1024,1024]{2,1,0:T(8,128)(2,1)}, u32[]{:S(2)}) copy-start(bf16[1,1024,1024]{2,1,0:T(8,128)(2,1)} %param.17) | copy-start | bytes 6291460
  2.6 25.2 %all-to-all-start.3 = ((bf16[8,32,1024]{2,1,0:T(8,128)(2,1)}), bf16[8,32,1024]{2,1,0:T(8,128)(2,1)S(1)}, u32[]{:S(2)}, u32[]{:S(2)}) async-start(bf16[8,32,1024]{2,1,0:T(8,128)(2,1)} %spread.3), calls=%async_computation.3 | async-start | bytes 1048576 | tf_op jit(solution)/shard_map/all_to_all | solution.py:121
  27.7 3.6 %copy-start.3 = (bf16[1,32,1024]{2,1,0:T(8,128)(2,1)S(1)}, bf16[1,32,1024]{2,1,0:T(8,128)(2,1)}, u32[]{:S(2)}) copy-start(bf16[1,32,1024]{2,1,0:T(8,128)(2,1)} %param.14) | copy-start | bytes 196612
  27.7 3.6 %copy-start.4 = (f32[1024]{0:T(1024)S(1)}, f32[1024]{0:T(1024)}, u32[]{:S(2)}) copy-start(f32[1024]{0:T(1024)} %param.16) | copy-start | bytes 12292
  31.4 47.3 %copy-start.1 = (bf16[1,1024,1024]{2,1,0:T(8,128)(2,1)S(1)}, bf16[1,1024,1024]{2,1,0:T(8,128)(2,1)}, u32[]{:S(2)}) copy-start(bf16[1,1024,1024]{2,1,0:T(8,128)(2,1)} %param.18) | copy-start | bytes 6291460
  31.4 4.1 %collective-permute-start.7 = (bf16[32,1024]{1,0:T(8,128)(2,1)S(1)}, bf16[32,1024]{1,0:T(8,128)(2,1)S(1)}, u32[]{:S(2)}, u32[]{:S(2)}) collective-permute-start(bf16[32,1024]{1,0:T(8,128)(2,1)S(1)} %get-tuple-element.118), channel_id=1, source_target_pairs={{448,960},{449,961},{450,962},{451,963},{452,964},{453,965},{454,9... | collective-permute-start | bytes 196616 | tf_op jit(solution)/shard_map/ppermute | solution.py:228
  32.2 4.0 %collective-permute-start.6 = (bf16[32,1024]{1,0:T(8,128)(2,1)S(1)}, bf16[32,1024]{1,0:T(8,128)(2,1)S(1)}, u32[]{:S(2)}, u32[]{:S(2)}) collective-permute-start(bf16[32,1024]{1,0:T(8,128)(2,1)S(1)} %get-tuple-element.118), channel_id=1, source_target_pairs={{448,896},{449,897},{450,898},{451,899},{452,900},{453,901},{454,9... | collective-permute-start | bytes 196616 | tf_op jit(solution)/shard_map/ppermute | solution.py:228
  32.9 25.6 %collective-permute-start.5 = (bf16[32,1024]{1,0:T(8,128)(2,1)S(1)}, bf16[32,1024]{1,0:T(8,128)(2,1)S(1)}, u32[]{:S(2)}, u32[]{:S(2)}) collective-permute-start(bf16[32,1024]{1,0:T(8,128)(2,1)S(1)} %get-tuple-element.118), channel_id=1, source_target_pairs={{448,512},{449,513},{450,514},{451,515},{452,516},{453,517},{454,5... | collective-permute-start | bytes 196616 | tf_op jit(solution)/shard_map/ppermute | solution.py:228
  34.2 44.4 %collective-permute-start.4 = (bf16[32,1024]{1,0:T(8,128)(2,1)S(1)}, bf16[32,1024]{1,0:T(8,128)(2,1)S(1)}, u32[]{:S(2)}, u32[]{:S(2)}) collective-permute-start(bf16[32,1024]{1,0:T(8,128)(2,1)S(1)} %get-tuple-element.118), channel_id=1, source_target_pairs={{448,832},{449,833},{450,834},{451,835},{452,836},{453,837},{454,8... | collective-permute-start | bytes 196616 | tf_op jit(solution)/shard_map/ppermute | solution.py:228
  34.9 43.7 %collective-permute-start.3 = (bf16[32,1024]{1,0:T(8,128)(2,1)S(1)}, bf16[32,1024]{1,0:T(8,128)(2,1)S(1)}, u32[]{:S(2)}, u32[]{:S(2)}) collective-permute-start(bf16[32,1024]{1,0:T(8,128)(2,1)S(1)} %get-tuple-element.118), channel_id=1, source_target_pairs={{448,576},{449,577},{450,578},{451,579},{452,580},{453,581},{454,5... | collective-permute-start | bytes 196616 | tf_op jit(solution)/shard_map/ppermute | solution.py:228
  35.6 43.1 %collective-permute-start.2 = (bf16[32,1024]{1,0:T(8,128)(2,1)S(1)}, bf16[32,1024]{1,0:T(8,128)(2,1)S(1)}, u32[]{:S(2)}, u32[]{:S(2)}) collective-permute-start(bf16[32,1024]{1,0:T(8,128)(2,1)S(1)} %get-tuple-element.118), channel_id=1, source_target_pairs={{448,768},{449,769},{450,770},{451,771},{452,772},{453,773},{454,7... | collective-permute-start | bytes 196616 | tf_op jit(solution)/shard_map/ppermute | solution.py:228
  36.3 42.4 %collective-permute-start.1 = (bf16[32,1024]{1,0:T(8,128)(2,1)S(1)}, bf16[32,1024]{1,0:T(8,128)(2,1)S(1)}, u32[]{:S(2)}, u32[]{:S(2)}) collective-permute-start(bf16[32,1024]{1,0:T(8,128)(2,1)S(1)} %get-tuple-element.118), channel_id=1, source_target_pairs={{448,704},{449,705},{450,706},{451,707},{452,708},{453,709},{454,7... | collective-permute-start | bytes 196616 | tf_op jit(solution)/shard_map/ppermute | solution.py:228
  58.5 20.2 %collective-permute-start = (bf16[32,1024]{1,0:T(8,128)(2,1)S(1)}, bf16[32,1024]{1,0:T(8,128)(2,1)S(1)}, u32[]{:S(2)}, u32[]{:S(2)}) collective-permute-start(bf16[32,1024]{1,0:T(8,128)(2,1)S(1)} %get-tuple-element.118), channel_id=1, source_target_pairs={{448,640},{449,641},{450,642},{451,643},{452,644},{453,645},{454,6... | collective-permute-start | bytes 196616 | tf_op jit(solution)/shard_map/ppermute | solution.py:228
  78.6 0.6 copy-start.5
  79.3 18.5 %copy-start.2 = (bf16[1024,1024]{1,0:T(8,128)(2,1)S(1)}, bf16[1024,1024]{1,0:T(8,128)(2,1)}, u32[]{:S(2)}) copy-start(bf16[1024,1024]{1,0:T(8,128)(2,1)} %get-tuple-element.108.w_value) | copy-start | bytes 6291460 | tf_op jit(solution)/shard_map/cond

commit v2 on v1

--- a/solution.py
+++ b/solution.py
@@ -27,56 +27,46 @@
 
 
 def attention_kernel(rows, w_query, w_key, w_value, w_out, cache, partial, made, kv, wk, wv, wo, queries, context, sems):
-    decoder = is_decoder()
-    encoder = jnp.logical_not(decoder)
     weights = [pltpu.make_async_copy(w_key, wk, sems.at[0]), pltpu.make_async_copy(w_value, wv, sems.at[1])]
     out_copy = pltpu.make_async_copy(w_out, wo, sems.at[2])
     kept = [pltpu.make_async_copy(cache.at[which], kv.at[which], sems.at[3 + which]) for which in range(2)]
     made_copies = [pltpu.make_async_copy(kv.at[which], made.at[which], sems.at[5 + which]) for which in range(2)]
 
+    def section(encoder):
+        for copy in weights if encoder else kept:
+            copy.start()
+        out_copy.start()
+        queries[...] = dot(rows[...], w_query[...]).astype(jnp.bfloat16)
+        for which, weight in enumerate((wk, wv)):
+            if encoder:
+                weights[which].wait()
+                kv[which] = dot(rows[...], weight[...]).astype(jnp.bfloat16)
+            else:
+                kept[which].wait()
+        for head in range(queries.shape[1] // HDIM):
+            cols = slice(head * HDIM, (head + 1) * HDIM)
+            scores = lax.dot_general(queries[:, cols], kv[0, :, cols], (((1,), (1,)), ((), ())), preferred_element_type=jnp.float32)
+            weight = jnp.exp(scores - jnp.max(scores, axis=-1, keepdims=True))
+            inverse = 1.0 / jnp.sum(weight, axis=-1, keepdims=True)
+            context[:, cols] = (dot(weight.astype(jnp.bfloat16), kv[1, :, cols]) * inverse).astype(jnp.bfloat16)
+        out_copy.wait()
+        if encoder:
+            for copy in made_copies:
+                copy.start()
+        partial[...] = dot(context[...], wo[...]).astype(jnp.bfloat16)
+        if encoder:
+            for copy in made_copies:
+                copy.wait()
+
+    decoder = is_decoder()
+
     @pl.when(decoder)
     def _():
-        for copy in kept:
-            copy.start()
-
-    @pl.when(encoder)
+        section(False)
+
+    @pl.when(jnp.logical_not(decoder))
     def _():
-        for copy in weights:
-            copy.start()
-
-    out_copy.start()
-    queries[...] = dot(rows[...], w_query[...]).astype(jnp.bfloat16)
-
-    @pl.when(decoder)
-    def _():
-        for copy in kept:
-            copy.wait()
-
-    @pl.when(encoder)
-    def _():
-        for which, weight in enumerate((wk, wv)):
-            weights[which].wait()
-            kv[which] = dot(rows[...], weight[...]).astype(jnp.bfloat16)
-
-    for head in range(queries.shape[1] // HDIM):
-        cols = slice(head * HDIM, (head + 1) * HDIM)
-        scores = lax.dot_general(queries[:, cols], kv[0, :, cols], (((1,), (1,)), ((), ())), preferred_element_type=jnp.float32)
-        weight = jnp.exp(scores - jnp.max(scores, axis=-1, keepdims=True))
-        inverse = 1.0 / jnp.sum(weight, axis=-1, keepdims=True)
-        context[:, cols] = (dot(weight.astype(jnp.bfloat16), kv[1, :, cols]) * inverse).astype(jnp.bfloat16)
-    out_copy.wait()
-
-    @pl.when(encoder)
-    def _():
-        for copy in made_copies:
-            copy.start()
-
-    partial[...] = dot(context[...], wo[...]).astype(jnp.bfloat16)
-
-    @pl.when(encoder)
-    def _():
-        for copy in made_copies:
-            copy.wait()
+        section(True)
 
 
 NEAR = pl.BlockSpec(memory_space=pltpu.VMEM)

time: 100 us -> 99.8 us (level)
  no operation moved by 1% of the time
where the time goes in v2:
time: 99.8 us; the launch traced here: 99.5 us
  waiting for transfers between devices  39.4 us (39%)
  blocking collectives  37.8 us (38%)
  starting transfers between devices  13.7 us (14%)
  Pallas kernels  6.99 us (7%)
    ppermute x8, waiting for transfers between devices, whole_section(): sends.append(lax.ppermute(memory_part, 'segment', [(half - 1, half + to)]))  21.9 us
    all_to_all x1, blocking collectives, arrive(): return lax.all_to_all(pieces, 'tensor', 0, 0, tiled=True)  19.4 us
    all_to_all x1, blocking collectives, gathered_copies(): return lax.all_to_all(copies, axis, 0, 0, tiled=True)  18.5 us
    all_to_all x1, waiting for transfers between devices, gathered_copies(): return lax.all_to_all(copies, axis, 0, 0, tiled=True)  17.5 us
    all_to_all x1, starting transfers between devices, gathered_copies(): return lax.all_to_all(copies, axis, 0, 0, tiled=True)  7.66 us
    ppermute x8, starting transfers between devices, whole_section(): sends.append(lax.ppermute(memory_part, 'segment', [(half - 1, half + to)]))  6.07 us
    pallas_call x1, Pallas kernels, attention(): pl.pallas_call(attention_kernel, out_shape=(jax.ShapeDtypeStruct((length,...  2.94 us
    pallas_call x1, Pallas kernels, memory_pair(): pl.pallas_call(memory_kernel, out_shape=jax.ShapeDtypeStruct(shape, memor...  2.01 us
  transfers between devices with their start and end apart: 9, of which 2 were waited for; matrix products, arithmetic and copies ran while one was open for 0% of the time, Pallas kernels for 0%

profile of v2, /device:TPU:896, one launch (start us, length us, event | category | flops | bytes accessed | tf_op | source)
XLA Modules:
  0.0 99.5 jit_solution(2055733358211688274)
XLA Ops:
  0.6 1.9 %spread.3 = bf16[8,32,1024]{2,1,0:T(8,128)(2,1)} custom-call(bf16[32,1024]{1,0:T(8,128)(2,1)} %bitcast.23, f32[1,1024]{1,0:T(1,128)} %gain.1), custom_call_target="tpu_custom_call" | custom-call | flops 20000000000 | bytes 1048576 | tf_op jit(solution)/shard_map/spread/pallas_call | solution.py:101
  2.6 7.7 %all-to-all-start.3 = ((bf16[8,32,1024]{2,1,0:T(8,128)(2,1)}), bf16[8,32,1024]{2,1,0:T(8,128)(2,1)S(1)}, u32[]{:S(2)}, u32[]{:S(2)}) async-start(bf16[8,32,1024]{2,1,0:T(8,128)(2,1)} %spread.3), calls=%async_computation.3 | async-start | bytes 1048576 | tf_op jit(solution)/shard_map/all_to_all | solution.py:111
  10.2 17.5 %all-to-all-done.3 = bf16[8,32,1024]{2,1,0:T(8,128)(2,1)S(1)} async-done(((bf16[8,32,1024]{2,1,0:T(8,128)(2,1)}), bf16[8,32,1024]{2,1,0:T(8,128)(2,1)S(1)}, u32[]{:S(2)}, u32[]{:S(2)}) %all-to-all-start.3) | async-done | bytes 524320 | tf_op jit(solution)/shard_map/all_to_all | solution.py:111
  27.7 2.9 %section_attention.1 = (bf16[256,1024]{1,0:T(8,128)(2,1)S(1)}, bf16[2,256,1024]{2,1,0:T(8,128)(2,1)}) custom-call(bf16[256,1024]{1,0:T(8,128)(2,1)S(1)} %bitcast.13, bf16[1024,1024]{1,0:T(8,128)(2,1)S(1)} %bitcast.12, bf16[1024,1024]{1,0:T(8,128)(2,1)} %bitcast.15, bf16[1024,1024]{1,0:T(8,128)(2,1)} %bitcast.17, bf16[1024,1024]{1,0:T(8,128)(2,1)} %bitcast.19, ...), custom_call_target="tpu_custom_call" | custom-call | tf_op jit(solution)/shard_map/section_attention/pallas_call | solution.py:118
  30.7 0.0 copy-start.1
  30.7 0.0 copy-done.3
  30.7 0.0 copy-done.4
  30.8 0.8 collective-permute-start.7
  31.6 0.7 collective-permute-start.6
  32.2 1.3 %collective-permute-start.5 = (bf16[32,1024]{1,0:T(8,128)(2,1)S(1)}, bf16[32,1024]{1,0:T(8,128)(2,1)S(1)}, u32[]{:S(2)}, u32[]{:S(2)}) collective-permute-start(bf16[32,1024]{1,0:T(8,128)(2,1)S(1)} %get-tuple-element.118), channel_id=1, source_target_pairs={{448,512},{449,513},{450,514},{451,515},{452,516},{453,517},{454,5... | collective-permute-start | bytes 196616 | tf_op jit(solution)/shard_map/ppermute | solution.py:218
  33.5 0.7 collective-permute-start.4
  34.2 0.7 collective-permute-start.3
  34.9 0.0 collective-permute-done.7
  34.9 0.7 collective-permute-start.2
  35.6 0.0 collective-permute-done.6
  35.6 0.7 collective-permute-start.1
  36.3 21.9 %collective-permute-done.5 = bf16[32,1024]{1,0:T(8,128)(2,1)S(1)} collective-permute-done((bf16[32,1024]{1,0:T(8,128)(2,1)S(1)}, bf16[32,1024]{1,0:T(8,128)(2,1)S(1)}, u32[]{:S(2)}, u32[]{:S(2)}) %collective-permute-start.5) | collective-permute-done | bytes 65568 | tf_op jit(solution)/shard_map/ppermute | solution.py:218
  58.1 0.7 collective-permute-start
  58.8 19.5 %conditional.4 = (bf16[32,1024]{1,0:T(8,128)(2,1)S(1)}) conditional(s32[]{:T(128)} %convert_element_type.2, bf16[32,1024]{1,0:T(8,128)(2,1)S(1)} %get-tuple-element.116, (bf16[8,32,1024]{2,1,0:T(8,128)(2,1)S(1)}, bf16[32,1024]{1,0:T(8,128)(2,1)S(1)}) %tuple.138), branch_computations={%region_2.0_spmd, %region_3.0_spmd} | conditional | bytes 1048584 | solution.py:219
  58.8 19.4 %all_to_all.18.arrived = bf16[8,32,1024]{2,1,0:T(8,128)(2,1)S(1)} all-to-all(bf16[8,32,1024]{2,1,0:T(8,128)(2,1)S(1)} %get-tuple-element.96), channel_id=1, replica_groups=mesh['segment'=16,'dp'=8,'tensor'=8] {'tensor'}, dimensions={0} | all-to-all | bytes 1048576 | tf_op jit(solution)/shard_map/cond/branch_1_fun/all_to_all | solution.py:213
  78.2 0.1 residual_only.1
  78.2 0.0 copy-start.5
  78.2 0.0 collective-permute-done.4
  78.3 0.0 collective-permute-done.3
  78.3 0.0 collective-permute-done.2
  78.3 0.0 collective-permute-done.1
  78.3 0.0 collective-permute-done
  78.3 0.6 copy-done.5
  78.9 20.6 %conditional.5 = (bf16[2,256,1024]{2,1,0:T(8,128)(2,1)}) conditional(s32[]{:T(128)} %convert_element_type.2, bf16[2,256,1024]{2,1,0:T(8,128)(2,1)} %get-tuple-element.117, (s32[]{:T(128)}, bf16[32,1024]{1,0:T(8,128)(2,1)S(1)}, bf16[32,1024]{1,0:T(8,128)(2,1)S(1)}, bf16[32,1024]{1,0:T(8,128)(2,1)S(1)}, bf16[32,1024]{1,0:T(8,128)(2,1)S(1)}, ...), branch_computations={%region_4.5_spmd, %region_5.6_spmd} | conditional | flops 20000229376 | bytes 11075690 | solution.py:228
  78.9 0.0 copy-start.2
  79.0 18.5 %all_to_all.19 = bf16[8,32,1024]{2,1,0:T(8,128)(2,1)S(1)} all-to-all(bf16[8,32,1024]{2,1,0:T(8,128)(2,1)S(1)} %spread.2), channel_id=1, replica_groups=mesh['segment'=16,'dp'=8,'tensor'=8] {'tensor'}, dimensions={0} | all-to-all | bytes 1048576 | tf_op jit(solution)/shard_map/cond/branch_1_fun/all_to_all | solution.py:111
  97.4 2.0 %memory_pair.1 = bf16[2,256,1024]{2,1,0:T(8,128)(2,1)} custom-call(bf16[256,1024]{1,0:T(8,128)(2,1)S(1)} %bitcast.14, bf16[1024,1024]{1,0:T(8,128)(2,1)S(1)} %get-tuple-element.107.w_key, bf16[1024,1024]{1,0:T(8,128)(2,1)S(1)} %copy-done.2), custom_call_target="tpu_custom_call" | custom-call | tf_op jit(solution)/shard_map/cond/branch_1_fun/memory_pair/pallas_call | solution.py:187
  (11 shorter events, 0.1 us)
Async XLA Ops:
  0.6 27.1 %copy-start = (bf16[1,1024,1024]{2,1,0:T(8,128)(2,1)S(1)}, bf16[1,1024,1024]{2,1,0:T(8,128)(2,1)}, u32[]{:S(2)}) copy-start(bf16[1,1024,1024]{2,1,0:T(8,128)(2,1)} %param.17) | copy-start | bytes 6291460
  2.6 25.2 %all-to-all-start.3 = ((bf16[8,32,1024]{2,1,0:T(8,128)(2,1)}), bf16[8,32,1024]{2,1,0:T(8,128)(2,1)S(1)}, u32[]{:S(2)}, u32[]{:S(2)}) async-start(bf16[8,32,1024]{2,1,0:T(8,128)(2,1)} %spread.3), calls=%async_computation.3 | async-start | bytes 1048576 | tf_op jit(solution)/shard_map/all_to_all | solution.py:111
  27.7 3.0 %copy-start.3 = (bf16[1,32,1024]{2,1,0:T(8,128)(2,1)S(1)}, bf16[1,32,1024]{2,1,0:T(8,128)(2,1)}, u32[]{:S(2)}) copy-start(bf16[1,32,1024]{2,1,0:T(8,128)(2,1)} %param.14) | copy-start | bytes 196612
  27.7 3.0 %copy-start.4 = (f32[1024]{0:T(1024)S(1)}, f32[1024]{0:T(1024)}, u32[]{:S(2)}) copy-start(f32[1024]{0:T(1024)} %param.16) | copy-start | bytes 12292
  30.7 47.6 %copy-start.1 = (bf16[1,1024,1024]{2,1,0:T(8,128)(2,1)S(1)}, bf16[1,1024,1024]{2,1,0:T(8,128)(2,1)}, u32[]{:S(2)}) copy-start(bf16[1,1024,1024]{2,1,0:T(8,128)(2,1)} %param.18) | copy-start | bytes 6291460
  30.8 4.1 %collective-permute-start.7 = (bf16[32,1024]{1,0:T(8,128)(2,1)S(1)}, bf16[32,1024]{1,0:T(8,128)(2,1)S(1)}, u32[]{:S(2)}, u32[]{:S(2)}) collective-permute-start(bf16[32,1024]{1,0:T(8,128)(2,1)S(1)} %get-tuple-element.118), channel_id=1, source_target_pairs={{448,960},{449,961},{450,962},{451,963},{452,964},{453,965},{454,9... | collective-permute-start | bytes 196616 | tf_op jit(solution)/shard_map/ppermute | solution.py:218
  31.6 4.0 %collective-permute-start.6 = (bf16[32,1024]{1,0:T(8,128)(2,1)S(1)}, bf16[32,1024]{1,0:T(8,128)(2,1)S(1)}, u32[]{:S(2)}, u32[]{:S(2)}) collective-permute-start(bf16[32,1024]{1,0:T(8,128)(2,1)S(1)} %get-tuple-element.118), channel_id=1, source_target_pairs={{448,896},{449,897},{450,898},{451,899},{452,900},{453,901},{454,9... | collective-permute-start | bytes 196616 | tf_op jit(solution)/shard_map/ppermute | solution.py:218
  32.2 25.9 %collective-permute-start.5 = (bf16[32,1024]{1,0:T(8,128)(2,1)S(1)}, bf16[32,1024]{1,0:T(8,128)(2,1)S(1)}, u32[]{:S(2)}, u32[]{:S(2)}) collective-permute-start(bf16[32,1024]{1,0:T(8,128)(2,1)S(1)} %get-tuple-element.118), channel_id=1, source_target_pairs={{448,512},{449,513},{450,514},{451,515},{452,516},{453,517},{454,5... | collective-permute-start | bytes 196616 | tf_op jit(solution)/shard_map/ppermute | solution.py:218
  33.5 44.7 %collective-permute-start.4 = (bf16[32,1024]{1,0:T(8,128)(2,1)S(1)}, bf16[32,1024]{1,0:T(8,128)(2,1)S(1)}, u32[]{:S(2)}, u32[]{:S(2)}) collective-permute-start(bf16[32,1024]{1,0:T(8,128)(2,1)S(1)} %get-tuple-element.118), channel_id=1, source_target_pairs={{448,832},{449,833},{450,834},{451,835},{452,836},{453,837},{454,8... | collective-permute-start | bytes 196616 | tf_op jit(solution)/shard_map/ppermute | solution.py:218
  34.2 44.0 %collective-permute-start.3 = (bf16[32,1024]{1,0:T(8,128)(2,1)S(1)}, bf16[32,1024]{1,0:T(8,128)(2,1)S(1)}, u32[]{:S(2)}, u32[]{:S(2)}) collective-permute-start(bf16[32,1024]{1,0:T(8,128)(2,1)S(1)} %get-tuple-element.118), channel_id=1, source_target_pairs={{448,576},{449,577},{450,578},{451,579},{452,580},{453,581},{454,5... | collective-permute-start | bytes 196616 | tf_op jit(solution)/shard_map/ppermute | solution.py:218
  34.9 43.4 %collective-permute-start.2 = (bf16[32,1024]{1,0:T(8,128)(2,1)S(1)}, bf16[32,1024]{1,0:T(8,128)(2,1)S(1)}, u32[]{:S(2)}, u32[]{:S(2)}) collective-permute-start(bf16[32,1024]{1,0:T(8,128)(2,1)S(1)} %get-tuple-element.118), channel_id=1, source_target_pairs={{448,768},{449,769},{450,770},{451,771},{452,772},{453,773},{454,7... | collective-permute-start | bytes 196616 | tf_op jit(solution)/shard_map/ppermute | solution.py:218
  35.6 42.7 %collective-permute-start.1 = (bf16[32,1024]{1,0:T(8,128)(2,1)S(1)}, bf16[32,1024]{1,0:T(8,128)(2,1)S(1)}, u32[]{:S(2)}, u32[]{:S(2)}) collective-permute-start(bf16[32,1024]{1,0:T(8,128)(2,1)S(1)} %get-tuple-element.118), channel_id=1, source_target_pairs={{448,704},{449,705},{450,706},{451,707},{452,708},{453,709},{454,7... | collective-permute-start | bytes 196616 | tf_op jit(solution)/shard_map/ppermute | solution.py:218
  58.1 20.2 %collective-permute-start = (bf16[32,1024]{1,0:T(8,128)(2,1)S(1)}, bf16[32,1024]{1,0:T(8,128)(2,1)S(1)}, u32[]{:S(2)}, u32[]{:S(2)}) collective-permute-start(bf16[32,1024]{1,0:T(8,128)(2,1)S(1)} %get-tuple-element.118), channel_id=1, source_target_pairs={{448,640},{449,641},{450,642},{451,643},{452,644},{453,645},{454,6... | collective-permute-start | bytes 196616 | tf_op jit(solution)/shard_map/ppermute | solution.py:218
  78.2 0.6 copy-start.5
  78.9 18.5 %copy-start.2 = (bf16[1024,1024]{1,0:T(8,128)(2,1)S(1)}, bf16[1024,1024]{1,0:T(8,128)(2,1)}, u32[]{:S(2)}) copy-start(bf16[1024,1024]{1,0:T(8,128)(2,1)} %get-tuple-element.108.w_value) | copy-start | bytes 6291460 | tf_op jit(solution)/shard_map/cond
